TPU v7x, 128 devices: a whole 4x4x4 slice. The times are simulated.
128 devices in a mesh: gx: 4 (over y), gy: 4 (over x_hi, core), gz: 8 (over z, x_lo).
Axes of the slice: x: 4 (x_hi: 2, x_lo: 2; x = x_hi * 2 + x_lo), y: 4, z: 4, core: 2. Of those that a mesh axis runs over, the one named last changes fastest.
Arguments:
- concentration: float32 [512, 512, 512], P('gz', 'gx', 'gy'), may hold values from -1 to 1
Outputs:
- concentration_next: float32 [512, 512, 512], P('gz', 'gx', 'gy')
All inputs are finite; a program needn't handle non-finite values.
Results may differ from a plain program's by a relative error of at most 0.00011.
Values sent between devices are 32-bit elements; how exact they have to be, the bound alone decides.
A program may use at most 192 MiB of HBM per device.

v0:
```python
import functools
import jax
import jax.numpy as jnp
from jax import lax
from jax.sharding import Mesh
from jax.sharding import PartitionSpec as P

GY = ("gy_0", "gy_1")
GZ = ("gz_0", "gz_1")
GX_GY_GZ = ("gx", "gy_0", "gy_1", "gz_0", "gz_1")
step_length = 0.2
stiffness = 0.25


def padded_2(x, sides, width):
    edges = {}
    for axis, dim in sides:
        count, length = (lax.axis_size(axis), x.shape[dim])
        up = [(i, (i + 1) % count) for i in range(count)]
        last = lax.slice_in_dim(x, length - width, length, axis=dim)
        leading = lax.slice_in_dim(x, 0, width, axis=dim)
        edges[dim] = (
            lax.ppermute(last, axis, up),
            lax.ppermute(leading, axis, [(b, a) for a, b in up]),
        )
    done = []
    for _, dim in sides:
        low, high = edges[dim]
        around = [(width, width) if d in done else (0, 0) for d in range(x.ndim)]
        x = jnp.concatenate([jnp.pad(low, around), x, jnp.pad(high, around)], axis=dim)
        done.append(dim)
    return x


def by_axis(x, axes):
    return functools.reduce(lax.psum, axes, x)


def hartley_table(length):
    indices = jnp.arange(length, dtype=jnp.int32)
    product = indices[:, None] * indices[None, :] % length
    angles = 2.0 * jnp.pi / length * product.astype(jnp.float32)
    return (jnp.cos(angles) + jnp.sin(angles)) / jnp.sqrt(float(length))


def wave_square(length):
    indices = jnp.arange(length, dtype=jnp.int32)
    folded = jnp.minimum(indices, length - indices).astype(jnp.float32)
    wave = 2.0 * jnp.pi / length * folded
    return wave * wave


def column_matmul(matrix, source):
    flat_columns = source.reshape(source.shape[0], -1)
    mapped = jnp.dot(
        matrix, flat_columns, precision=lax.Precision.HIGHEST, preferred_element_type=jnp.float32
    )
    return mapped.reshape(source.shape)


def plane_pass(planes, hartley_x, hartley_y):
    mapped = jnp.einsum("ij,rjy->riy", hartley_x, planes, precision=lax.Precision.HIGHEST)
    flat_planes = mapped.reshape(-1, planes.shape[2])
    mapped = jnp.dot(
        flat_planes,
        hartley_y.T,
        precision=lax.Precision.HIGHEST,
        preferred_element_type=jnp.float32,
    )
    return mapped.reshape(planes.shape)


def face_terms(padded_pot, padded_mob, axis_number):
    length = padded_pot.shape[axis_number]
    lower_pot = lax.slice_in_dim(padded_pot, 0, length - 1, axis=axis_number)
    upper_pot = lax.slice_in_dim(padded_pot, 1, length, axis=axis_number)
    lower_mob = lax.slice_in_dim(padded_mob, 0, length - 1, axis=axis_number)
    upper_mob = lax.slice_in_dim(padded_mob, 1, length, axis=axis_number)
    flux = 0.5 * (lower_mob + upper_mob) * (upper_pot - lower_pot)
    count = flux.shape[axis_number]
    return lax.slice_in_dim(flux, 1, count, axis=axis_number) - lax.slice_in_dim(
        flux, 0, count - 1, axis=axis_number
    )


def solve_planes(planes, hartley_x, hartley_y, local_z, wave_x, wave_y, mean_mobility):
    planes = plane_pass(planes, hartley_x, hartley_y)
    wave_sum = local_z[:, None, None] + wave_x[None, :, None] + wave_y[None, None, :]
    planes = planes / (1.0 + step_length * stiffness * mean_mobility * wave_sum * wave_sum)
    return plane_pass(planes, hartley_x, hartley_y)


def local(concentration):
    block_z, block_x, block_y = concentration.shape
    groups_x = lax.axis_size("gx")
    groups_y = lax.axis_size(GY)
    groups_z = lax.axis_size(GZ)
    whole_z = block_z * groups_z
    whole_x = block_x * groups_x
    whole_y = block_y * groups_y
    hartley_z = hartley_table(whole_z)
    hartley_x = hartley_table(whole_x)
    hartley_y = hartley_table(whole_y)
    padded = padded_2(concentration, (("gx", 1), (GY, 2), (GZ, 0)), 1)
    padded_pot = padded * padded * padded - padded
    padded_mob = 1.05 - padded * padded
    mobility = padded_mob[1:-1, 1:-1, 1:-1]
    mobility_sum = by_axis(jnp.sum(mobility), GX_GY_GZ)
    mean_mobility = mobility_sum / (whole_x * whole_y * whole_z)
    divergence = face_terms(padded_pot[:, 1:-1, 1:-1], padded_mob[:, 1:-1, 1:-1], 0)
    divergence = divergence + face_terms(padded_pot[1:-1, :, 1:-1], padded_mob[1:-1, :, 1:-1], 1)
    divergence = divergence + face_terms(padded_pot[1:-1, 1:-1, :], padded_mob[1:-1, 1:-1, :], 2)
    update = concentration + step_length * divergence
    wave_z = wave_square(whole_z)
    wave_x = wave_square(whole_x)
    wave_y = wave_square(whole_y)
    devices = groups_x * groups_y * groups_z
    rows_each = whole_z // devices
    slim_x = block_x // groups_z
    member = (lax.axis_index("gx") * groups_y + lax.axis_index(GY)) * groups_z + lax.axis_index(GZ)
    pencil = lax.all_to_all(update, GZ, split_axis=1, concat_axis=0, tiled=True)
    pencil = column_matmul(hartley_z, pencil)
    outgoing = pencil.reshape(devices, rows_each, slim_x, block_y)
    received = lax.all_to_all(outgoing, GX_GY_GZ, split_axis=0, concat_axis=0, tiled=True)
    planes = received.reshape(groups_x, groups_y, groups_z, rows_each, slim_x, block_y)
    planes = planes.transpose(3, 0, 2, 4, 1, 5).reshape(rows_each, whole_x, whole_y)
    local_z = lax.dynamic_slice_in_dim(wave_z, member * rows_each, rows_each, 0)
    planes = solve_planes(planes, hartley_x, hartley_y, local_z, wave_x, wave_y, mean_mobility)
    returning = planes.reshape(rows_each, groups_x, groups_z, slim_x, groups_y, block_y)
    returning = returning.transpose(1, 4, 2, 0, 3, 5).reshape(devices, rows_each, slim_x, block_y)
    arrived = lax.all_to_all(returning, GX_GY_GZ, split_axis=0, concat_axis=0, tiled=True)
    pencil = column_matmul(hartley_z, arrived.reshape(whole_z, slim_x, block_y))
    return lax.all_to_all(pencil, GZ, split_axis=0, concat_axis=1, tiled=True)


def solution(mesh):
    torus = Mesh(
        mesh.devices.reshape(mesh.shape["gx"], 2, 2, 4, 2), ("gx", "gy_0", "gy_1", "gz_0", "gz_1")
    )
    in_specs = (P(GZ, "gx", GY),)
    out_specs = P(GZ, "gx", GY)
    return jax.shard_map(local, mesh=torus, in_specs=in_specs, out_specs=out_specs, check_vma=False)
```

profile of v0, /device:TPU:0, one launch (start us, length us, event | category | flops | bytes accessed | tf_op | source)
XLA Modules:
  0.0 495.5 jit_solution(6628184515026197495)
XLA Ops:
  0.0 8.1 %fusion.113 = (f32[64,128,1]{2,1,0:T(8,128)}, f32[64,128,1]{2,1,0:T(8,128)}) fusion(f32[64,128,128]{2,1,0:T(8,128)} %param.1), kind=kLoop, calls=%fused_computation.146 | loop fusion | bytes 131072 | tf_op jit(solution)/shard_map/slice | solution.py:20
  8.1 2.8 copy.35
  11.0 0.9 fusion.112
  11.9 1.7 collective-permute-start
  13.6 3.6 collective-permute-start.5
  17.1 4.6 copy.19
  21.8 1.9 copy-done.1
  23.7 1.6 collective-permute-start.2
  25.3 2.8 copy.36
  28.1 3.3 collective-permute-start.4
  31.4 1.9 collective-permute-start.3
  33.3 4.4 copy.37
  37.8 4.4 copy.38
  42.2 12.8 %multiply_subtract_fusion.1 = (f32[66,130,130]{2,0,1:T(8,128)S(1)}, f32[66,130,130]{2,0,1:T(8,128)}) fusion(f32[1,128,128]{2,0,1:T(1,128)S(1)} %collective-permute-done.5, f32[64,128,1]{2,0,1:T(8,128)} %copy.38, f32[64,1,128]{2,0,1:T(8,128)S(1)} %collective-permute-done.3, f32[64,128,128]{2,0,1:T(8,128)} %copy-done.1, ...), kind=kLoop, calls=%fused_computation.3 | loop fusion | flops 27885000 | bytes 13379648 | tf_op jit(solution)/shard_map/sub | solution.py:106
  55.0 14.1 %fusion.6 = f32[65,128,128]{2,0,1:T(8,128)} fusion(f32[66,130,130]{2,0,1:T(8,128)} %get-tuple-element.6, f32[66,130,130]{2,0,1:T(8,128)S(1)} %get-tuple-element.5), kind=kLoop, calls=%fused_computation.21 | loop fusion | flops 4259840 | bytes 21299200 | tf_op jit(solution)/shard_map/mul | solution.py:79
  69.1 10.4 %fusion.8 = f32[64,129,128]{2,0,1:T(8,128)} fusion(f32[66,130,130]{2,0,1:T(8,128)} %get-tuple-element.6, f32[66,130,130]{2,0,1:T(8,128)S(1)} %get-tuple-element.5), kind=kLoop, calls=%fused_computation.25 | loop fusion | flops 4227072 | bytes 21135360 | tf_op jit(solution)/shard_map/mul | solution.py:79
  79.5 15.3 %fusion.4 = f32[64,128,129]{2,0,1:T(8,128)} fusion(f32[66,130,130]{2,0,1:T(8,128)} %get-tuple-element.6, f32[66,130,130]{2,0,1:T(8,128)S(1)} %get-tuple-element.5), kind=kLoop, calls=%fused_computation.16 | loop fusion | flops 4227072 | bytes 21135360 | tf_op jit(solution)/shard_map/mul | solution.py:79
  94.7 14.9 %fusion.16 = f32[64,128,128]{2,0,1:T(8,128)} fusion(f32[64,128,129]{2,0,1:T(8,128)} %fusion.4, f32[64,129,128]{2,0,1:T(8,128)} %fusion.8, f32[65,128,128]{2,0,1:T(8,128)} %fusion.6, f32[64,128,128]{2,1,0:T(8,128)} %param.1), kind=kLoop, calls=%fused_computation.37 | loop fusion | flops 7340032 | bytes 33554432 | tf_op jit(solution)/shard_map/add | solution.py:113
  109.7 4.6 all-to-all-start
  114.2 48.1 %all-to-all-done = f32[64,128,128]{2,0,1:T(8,128)} async-done(((f32[64,128,128]{2,0,1:T(8,128)}), f32[64,128,128]{2,0,1:T(8,128)}, u32[]{:S(2)}, u32[]{:S(2)}) %all-to-all-start) | async-done | bytes 4194336 | tf_op jit(solution)/shard_map/all_to_all | solution.py:121
  162.4 4.6 copy.20
  166.9 4.0 copy.46
  170.9 5.8 %copy.21 = f32[2048,512]{1,0:T(8,128)} copy(f32[2048,512]{0,1:T(8,128)} %bitcast.74) | data formatting | bytes 8388608 | tf_op jit(solution)/shard_map/dot_general | solution.py:55
  176.7 13.2 %fusion.35 = f32[128,4,16,128]{3,0,2,1:T(8,128)S(1)} fusion(f32[16,128,512,1]{2,1,0,3:T(8,128)} %bitcast.72, s32[128,4]{0,1:T(4,128)S(1)} %multiply_add_fusion.1), kind=kOutput, calls=%fused_computation.69 | convolution fusion | flops 6446645248 | bytes 8390656 | tf_op jit(solution)/shard_map/dot_general | solution.py:55
  189.9 4.6 copy.22
  194.6 6.7 %all-to-all-start.1 = ((f32[128,4,16,128]{3,2,1,0:T(8,128)}), f32[128,4,16,128]{3,2,1,0:T(8,128)}, u32[]{:S(2)}, u32[]{:S(2)}) async-start(f32[128,4,16,128]{3,2,1,0:T(8,128)} %copy.22), calls=%async_computation.1 | async-start | bytes 8388608 | tf_op jit(solution)/shard_map/all_to_all | solution.py:124
  201.3 5.4 %slice_reduce_fusion = f32[]{:T(128)} fusion(f32[66,130,130]{2,0,1:T(8,128)} %copy-done), kind=kLoop, calls=%fused_computation.33 | loop fusion | flops 1048575 | bytes 4194308 | tf_op jit(solution)/shard_map/reduce_sum | solution.py:108
  206.8 43.6 %psum.35 = f32[]{:T(128)} all-reduce(f32[]{:T(128)} %slice_reduce_fusion), channel_id=1, replica_groups=mesh['gx'=4,'gy_0'=2,'gy_1'=2,'gz_0'=4,'gz_1'=2] {'gx'}, use_global_device_ids=true, to_apply=%region_1.2 | all-reduce | flops 1 | bytes 8 | tf_op jit(solution)/shard_map/psum | solution.py:36
  250.3 7.0 %psum.36 = f32[]{:T(128)} all-reduce(f32[]{:T(128)} %psum.35), channel_id=1, replica_groups=mesh['gx'=4,'gy_0'=2,'gy_1'=2,'gz_0'=4,'gz_1'=2] {'gy_0'}, use_global_device_ids=true, to_apply=%region_2.3 | all-reduce | flops 1 | bytes 8 | tf_op jit(solution)/shard_map/psum | solution.py:36
  257.4 0.1 dynamic_slice.3
  257.4 3.1 psum.37
  260.5 0.1 broadcast_add_fusion
  260.6 12.4 %psum.38 = f32[]{:T(128)} all-reduce(f32[]{:T(128)} %psum.37), channel_id=1, replica_groups=mesh['gx'=4,'gy_0'=2,'gy_1'=2,'gz_0'=4,'gz_1'=2] {'gz_0'}, use_global_device_ids=true, to_apply=%region_4.5 | all-reduce | flops 1 | bytes 8 | tf_op jit(solution)/shard_map/psum | solution.py:36
  273.0 5.5 %psum.39 = f32[]{:T(128)} all-reduce(f32[]{:T(128)} %psum.38), channel_id=1, replica_groups=mesh['gx'=4,'gy_0'=2,'gy_1'=2,'gz_0'=4,'gz_1'=2] {'gz_1'}, use_global_device_ids=true, to_apply=%region_5.6 | all-reduce | flops 1 | bytes 8 | tf_op jit(solution)/shard_map/psum | solution.py:36
  279.2 6.9 %copy.47 = f32[4,4,8,4,16,128]{5,1,4,2,0,3:T(4,128)} copy(f32[4,4,8,4,16,128]{5,4,3,2,1,0:T(8,128)} %bitcast.11) | data formatting | bytes 8388608 | tf_op jit(solution)/shard_map/reshape | solution.py:125
  286.1 5.5 %reshape.232 = f32[4,512,512]{2,1,0:T(8,128)} reshape(f32[4,4,8,16,4,128]{5,4,3,2,1,0:T(4,128)} %bitcast.75) | data formatting | bytes 8388608 | tf_op jit(solution)/shard_map/reshape | solution.py:126
  291.5 20.3 %fusion.41 = f32[4,512,512]{2,1,0:T(8,128)S(1)} fusion(f32[4,512,512]{2,1,0:T(8,128)} %reshape.232), kind=kOutput, calls=%fused_computation.75 | convolution fusion | flops 6446645248 | bytes 8388608 | tf_op jit(solution)/shard_map/ij,rjy->riy/dot_general | solution.py:62
  311.8 19.9 %fusion.18 = f32[4,512,512]{2,1,0:T(8,128)S(1)} fusion(f32[4,512,512]{2,1,0:T(8,128)S(1)} %fusion.41), kind=kOutput, calls=%fused_computation.41 | convolution fusion | flops 6446645248 | bytes 8388608 | tf_op jit(solution)/shard_map/dot_general | solution.py:64
  331.7 13.4 %fusion.12 = f32[4,512,512]{1,2,0:T(8,128)S(1)} fusion(f32[4,512,512]{2,1,0:T(8,128)S(1)} %fusion.18, f32[512]{0:T(512)S(1)} %fusion.80, f32[4,512]{1,0:T(4,128)S(1)} %broadcast_add_fusion, f32[]{:T(128)S(6)} %mul_shard_map.3), kind=kOutput, calls=%fused_computation.30 | convolution fusion | flops 6451888128 | bytes 8398852 | tf_op jit(solution)/shard_map/ij,rjy->riy/dot_general | solution.py:62
  345.1 11.1 %convolution_bitcast_fusion = f32[4,4,8,4,16,128]{5,4,1,2,0,3:T(8,128)S(1)} fusion(f32[4,4,8,16,512,1]{4,3,5,2,1,0:T(8,128)S(1)} %bitcast.80, s32[4,128]{1,0:T(4,128)S(1)} %multiply_add_fusion), kind=kOutput, calls=%fused_computation.45 | convolution fusion | flops 6446645248 | bytes 8390656 | tf_op jit(solution)/shard_map/dot_general | solution.py:64
  356.2 0.6 copy.26
  356.8 59.6 %all_to_all.43 = f32[128,4,16,128]{3,2,1,0:T(8,128)S(1)} all-to-all(f32[128,4,16,128]{3,2,1,0:T(8,128)S(1)} %bitcast.76), channel_id=1, replica_groups=mesh['gx'=4,'gy_0'=2,'gy_1'=2,'gz_0'=4,'gz_1'=2] {'gx','gy_0','gy_1','gz..., dimensions={0} | all-to-all | bytes 8388608 | tf_op jit(solution)/shard_map/all_to_all | solution.py:131
  416.5 4.0 copy.45
  420.4 5.5 %copy.27 = f32[2048,512]{1,0:T(8,128)} copy(f32[2048,512]{0,1:T(8,128)} %bitcast.78) | data formatting | bytes 8388608 | tf_op jit(solution)/shard_map/dot_general | solution.py:55
  425.9 13.2 %fusion.37 = f32[512,16,128]{2,0,1:T(8,128)S(1)} fusion(f32[16,128,512]{2,1,0:T(8,128)} %bitcast.71), kind=kOutput, calls=%fused_computation.71 | convolution fusion | flops 6446645248 | bytes 8388608 | tf_op jit(solution)/shard_map/dot_general | solution.py:55
  439.1 2.4 copy.28
  441.5 51.2 %all_to_all.44 = f32[512,16,128]{2,1,0:T(8,128)S(1)} all-to-all(f32[512,16,128]{2,1,0:T(8,128)S(1)} %copy.28), channel_id=1, replica_groups=mesh['gx'=4,'gy_0'=2,'gy_1'=2,'gz_0'=4,'gz_1'=2] {'gz_0','gz_1'}, dimensions={0} | all-to-all | bytes 8388608 | tf_op jit(solution)/shard_map/all_to_all | solution.py:133
  492.7 2.6 copy.29
  (15 shorter events, 0.1 us)
Async XLA Ops:
  10.9 20.5 %collective-permute-start.1 = (f32[64,128,1]{1,0,2:T(8,128)S(1)}, f32[64,128,1]{1,0,2:T(8,128)S(1)}, u32[]{:S(2)}, u32[]{:S(2)}) collective-permute-start(f32[64,128,1]{1,0,2:T(8,128)S(1)} %copy.35), channel_id=1, source_target_pairs={{0,8},{8,16},{16,24},{24,0},{1,9},{9,17},{17,25},{25,1},{2,10},{10... | collective-permute-start | bytes 98312 | tf_op jit(solution)/shard_map/ppermute | solution.py:23
  11.9 30.3 %collective-permute-start = (f32[1,128,128]{2,0,1:T(1,128)S(1)}, f32[1,128,128]{2,0,1:T(1,128)S(1)}, u32[]{:S(2)}, u32[]{:S(2)}) collective-permute-start(f32[1,128,128]{2,0,1:T(1,128)S(1)} %bitcast.82), channel_id=1, source_target_pairs={{0,1},{1,2},{2,3},{3,4},{4,5},{5,6},{6,7},{7,0},{8,9},{9,10},{10,1... | collective-permute-start | bytes 196616 | tf_op jit(solution)/shard_map/ppermute | solution.py:23
  13.6 28.6 %collective-permute-start.5 = (f32[1,128,128]{2,0,1:T(1,128)S(1)}, f32[1,128,128]{2,0,1:T(1,128)S(1)}, u32[]{:S(2)}, u32[]{:S(2)}) collective-permute-start(f32[1,128,128]{2,0,1:T(1,128)S(1)} %bitcast.81), channel_id=1, source_target_pairs={{1,0},{2,1},{3,2},{4,3},{5,4},{6,5},{7,6},{0,7},{9,8},{10,9},{11,1... | collective-permute-start | bytes 196616 | tf_op jit(solution)/shard_map/ppermute | solution.py:24
  21.7 1.9 copy-start.1
  23.7 18.5 %collective-permute-start.2 = (f32[64,1,128]{2,0,1:T(8,128)S(1)}, f32[64,1,128]{2,0,1:T(8,128)S(1)}, u32[]{:S(2)}, u32[]{:S(2)}) collective-permute-start(f32[64,1,128]{2,0,1:T(8,128)S(1)} %get-tuple-element.11), channel_id=1, source_target_pairs={{0,32},{32,64},{64,96},{96,0},{1,33},{33,65},{65,97},{97,1},{2,34}... | collective-permute-start | bytes 98312 | tf_op jit(solution)/shard_map/ppermute | solution.py:23
  28.1 9.7 %collective-permute-start.4 = (f32[64,128,1]{1,0,2:T(8,128)S(1)}, f32[64,128,1]{1,0,2:T(8,128)S(1)}, u32[]{:S(2)}, u32[]{:S(2)}) collective-permute-start(f32[64,128,1]{1,0,2:T(8,128)S(1)} %copy.36), channel_id=1, source_target_pairs={{8,0},{16,8},{24,16},{0,24},{9,1},{17,9},{25,17},{1,25},{10,2},{18... | collective-permute-start | bytes 98312 | tf_op jit(solution)/shard_map/ppermute | solution.py:24
  31.4 10.7 %collective-permute-start.3 = (f32[64,1,128]{2,0,1:T(8,128)S(1)}, f32[64,1,128]{2,0,1:T(8,128)S(1)}, u32[]{:S(2)}, u32[]{:S(2)}) collective-permute-start(f32[64,1,128]{2,0,1:T(8,128)S(1)} %get-tuple-element.12), channel_id=1, source_target_pairs={{32,0},{64,32},{96,64},{0,96},{33,1},{65,33},{97,65},{1,97},{34,2}... | collective-permute-start | bytes 98312 | tf_op jit(solution)/shard_map/ppermute | solution.py:24
  54.9 24.5 %copy-start = (f32[66,130,130]{2,0,1:T(8,128)}, f32[66,130,130]{2,0,1:T(8,128)S(1)}, u32[]{:S(2)}) copy-start(f32[66,130,130]{2,0,1:T(8,128)S(1)} %get-tuple-element.5) | copy-start | bytes 13384804
  109.7 52.7 %all-to-all-start = ((f32[64,128,128]{2,0,1:T(8,128)}), f32[64,128,128]{2,0,1:T(8,128)}, u32[]{:S(2)}, u32[]{:S(2)}) async-start(f32[64,128,128]{2,0,1:T(8,128)} %fusion.16), calls=%async_computation | async-start | bytes 8388608 | tf_op jit(solution)/shard_map/all_to_all | solution.py:121
  194.6 84.6 %all-to-all-start.1 = ((f32[128,4,16,128]{3,2,1,0:T(8,128)}), f32[128,4,16,128]{3,2,1,0:T(8,128)}, u32[]{:S(2)}, u32[]{:S(2)}) async-start(f32[128,4,16,128]{3,2,1,0:T(8,128)} %copy.22), calls=%async_computation.1 | async-start | bytes 8388608 | tf_op jit(solution)/shard_map/all_to_all | solution.py:124
where the time goes:
time: 502 us; the launch traced here: 496 us
  blocking collectives  182 us (36%)
  matrix products  91 us (18%)
  local copies, waits for them, and re-layouts  76.6 us (15%)
  other arithmetic  73 us (15%)
  waiting for transfers between devices  48.1 us (10%)
  starting transfers between devices  23.4 us (5%)
    psum x5, blocking collectives, by_axis(): return functools.reduce(lax.psum, axes, x)  71.7 us
    all_to_all x1, blocking collectives, local(): lax.all_to_all(returning, GX_GY_GZ, split_axis=0, concat_axis=0, tiled=True)  59.6 us
    all_to_all x1, blocking collectives, local(): return lax.all_to_all(pencil, GZ, split_axis=0, concat_axis=1, tiled=True)  51.2 us
    all_to_all x1, waiting for transfers between devices, local(): pencil = lax.all_to_all(update, GZ, split_axis=1, concat_axis=0, tiled=True)  48.1 us
    mul x3, other arithmetic, face_terms(): flux = 0.5 * (lower_mob + upper_mob) * (upper_pot - lower_pot)  39.8 us
    dot_general x2, matrix products, plane_pass(): jnp.einsum('ij,rjy->riy', hartley_x, planes, precision=lax.Precision.HIGH...  33.7 us
    dot_general x2, matrix products, plane_pass(): jnp.dot(flat_planes, hartley_y.T, precision=lax.Precision.HIGHEST, prefer...  31 us
    unnamed x11, local copies, waits for them, and re-layouts  29 us
  transfers between devices with their start and end apart: 8, of which 1 were waited for; matrix products, arithmetic and copies ran while one was open for 5% of the time, Pallas kernels for 0%

commit v1 on v0

--- a/solution.py
+++ b/solution.py
@@ -118,7 +118,10 @@
     rows_each = whole_z // devices
     slim_x = block_x // groups_z
     member = (lax.axis_index("gx") * groups_y + lax.axis_index(GY)) * groups_z + lax.axis_index(GZ)
-    pencil = lax.all_to_all(update, GZ, split_axis=1, concat_axis=0, tiled=True)
+    pencil = jnp.concatenate(
+        jax.lax.all_to_all(jnp.stack(jnp.split(update, jax.lax.axis_size(GZ), axis=1)), GZ, 0, 0),
+        axis=0,
+    )
     pencil = column_matmul(hartley_z, pencil)
     outgoing = pencil.reshape(devices, rows_each, slim_x, block_y)
     received = lax.all_to_all(outgoing, GX_GY_GZ, split_axis=0, concat_axis=0, tiled=True)

time: 502 us -> 507 us (level)
  other arithmetic: 73 us -> 84.2 us
    sub x0 -> x1, other arithmetic: none -> 11.5 us  [local(): padded_pot = padded * padded * padded - padded]
    another operation x0 -> x2, local copies, waits for them, and re-layouts: none -> 6.39 us  [the longest x1 5.56 us: column_matmul(): flat_columns = source.reshape(source.shape[0], -1)]
    dot_general x4 -> x3, local copies, waits for them, and re-layouts: 18.4 us -> 12.8 us  [column_matmul(): jnp.dot(matrix, flat_columns, precision=lax.Precision.HIGHEST, preferred_...]
    unnamed x11 -> x15, local copies, waits for them, and re-layouts: 29 us -> 26.9 us
  transfers between devices with their start and end apart: 8 -> 8, of which waited for: 1 -> 1; matrix products, arithmetic and copies ran while one was open for 5% -> 3% of each run, Pallas kernels for 0% -> 0%
where the time goes in v1:
time: 507 us; the launch traced here: 502 us
  blocking collectives  183 us (36%)
  matrix products  90.8 us (18%)
  other arithmetic  84.2 us (17%)
  local copies, waits for them, and re-layouts  71.8 us (14%)
  waiting for transfers between devices  48.2 us (10%)
  starting transfers between devices  23.4 us (5%)
    psum x5, blocking collectives, by_axis(): return functools.reduce(lax.psum, axes, x)  71.8 us
    all_to_all x1, blocking collectives, local(): lax.all_to_all(returning, GX_GY_GZ, split_axis=0, concat_axis=0, tiled=True)  59.6 us
    all_to_all x1, blocking collectives, local(): return lax.all_to_all(pencil, GZ, split_axis=0, concat_axis=1, tiled=True)  51.2 us
    all_to_all x1, waiting for transfers between devices, local(): jax.lax.all_to_all(jnp.stack(jnp.split(update, jax.lax.axis_size(GZ), axi...  48.2 us
    mul x3, other arithmetic, face_terms(): flux = 0.5 * (lower_mob + upper_mob) * (upper_pot - lower_pot)  39.3 us
    dot_general x2, matrix products, plane_pass(): jnp.einsum('ij,rjy->riy', hartley_x, planes, precision=lax.Precision.HIGH...  33.2 us
    dot_general x2, matrix products, plane_pass(): jnp.dot(flat_planes, hartley_y.T, precision=lax.Precision.HIGHEST, prefer...  31.2 us
    unnamed x15, local copies, waits for them, and re-layouts  26.9 us
  transfers between devices with their start and end apart: 8, of which 1 were waited for; matrix products, arithmetic and copies ran while one was open for 3% of the time, Pallas kernels for 0%

profile of v1, /device:TPU:0, one launch (start us, length us, event | category | flops | bytes accessed | tf_op | source)
XLA Modules:
  0.0 502.0 jit_solution(17537794128075092280)
XLA Ops:
  0.0 8.1 %fusion.121 = (f32[64,128,1]{2,1,0:T(8,128)}, f32[64,128,1]{2,1,0:T(8,128)}) fusion(f32[64,128,128]{2,1,0:T(8,128)} %param.1), kind=kLoop, calls=%fused_computation.162 | loop fusion | bytes 131072 | tf_op jit(solution)/shard_map/slice | solution.py:20
  8.1 2.8 copy.27
  11.0 2.8 copy.28
  13.8 3.3 collective-permute-start.4
  17.1 0.9 fusion.120
  18.0 1.7 collective-permute-start
  19.7 3.6 collective-permute-start.5
  23.2 1.1 fusion.122
  24.3 1.6 collective-permute-start.2
  25.9 1.9 collective-permute-start.3
  27.9 2.6 copy.29
  30.5 2.7 copy.30
  33.2 15.8 %multiply_subtract_fusion.1 = (f32[66,130,130]{2,1,0:T(8,128)S(1)}, f32[66,130,130]{2,1,0:T(8,128)}) fusion(f32[1,128,128]{2,1,0:T(8,128)S(1)} %collective-permute-done.5, f32[64,128,1]{2,1,0:T(8,128)} %copy.30, f32[64,1,128]{2,1,0:T(1,128)S(1)} %collective-permute-done.3, f32[64,128,128]{2,1,0:T(8,128)} %param.1, ...), kind=kLoop, calls=%fused_computation.3 | loop fusion | flops 25654200 | bytes 13379648 | tf_op jit(solution)/shard_map/sub | solution.py:106
  48.9 11.5 %multiply_subtract_fusion = f32[66,130,130]{2,1,0:T(8,128)} fusion(f32[66,130,130]{2,1,0:T(8,128)} %get-tuple-element.6), kind=kLoop, calls=%fused_computation.2 | loop fusion | flops 3346200 | bytes 8923200 | tf_op jit(solution)/shard_map/sub | solution.py:105
  60.4 9.9 %fusion.8 = f32[65,128,128]{2,1,0:T(8,128)} fusion(f32[66,130,130]{2,1,0:T(8,128)} %multiply_subtract_fusion, f32[66,130,130]{2,1,0:T(8,128)S(1)} %get-tuple-element.5), kind=kLoop, calls=%fused_computation.25 | loop fusion | flops 4259840 | bytes 21299200 | tf_op jit(solution)/shard_map/mul | solution.py:79
  70.4 13.4 %fusion.6 = f32[64,129,128]{2,1,0:T(8,128)} fusion(f32[66,130,130]{2,1,0:T(8,128)} %multiply_subtract_fusion, f32[66,130,130]{2,1,0:T(8,128)S(1)} %get-tuple-element.5), kind=kLoop, calls=%fused_computation.21 | loop fusion | flops 4227072 | bytes 21135360 | tf_op jit(solution)/shard_map/mul | solution.py:79
  83.7 16.0 %fusion.4 = f32[64,128,129]{2,1,0:T(8,128)} fusion(f32[66,130,130]{2,1,0:T(8,128)} %multiply_subtract_fusion, f32[66,130,130]{2,1,0:T(8,128)S(1)} %get-tuple-element.5), kind=kLoop, calls=%fused_computation.16 | loop fusion | flops 4227072 | bytes 21135360 | tf_op jit(solution)/shard_map/mul | solution.py:79
  99.7 12.3 %fusion.16 = f32[64,128,128]{2,1,0:T(8,128)S(1)} fusion(f32[64,128,128]{2,1,0:T(8,128)} %param.1, f32[64,128,129]{2,1,0:T(8,128)} %fusion.4, f32[64,129,128]{2,1,0:T(8,128)} %fusion.6, f32[65,128,128]{2,1,0:T(8,128)} %fusion.8), kind=kLoop, calls=%fused_computation.37 | loop fusion | flops 7340032 | bytes 33554432 | tf_op jit(solution)/shard_map/add | solution.py:113
  112.0 0.8 fusion.73
  112.8 0.8 fusion.72
  113.7 0.8 fusion.71
  114.5 0.8 fusion.70
  118.7 4.6 all-to-all-start
  123.3 48.2 %all-to-all-done = f32[8,64,16,128]{3,2,1,0:T(8,128)} async-done(((f32[8,64,16,128]{3,2,1,0:T(8,128)}), f32[8,64,16,128]{3,2,1,0:T(8,128)}, u32[]{:S(2)}, u32[]{:S(2)}) %all-to-all-start) | async-done | bytes 4194336 | tf_op jit(solution)/shard_map/all_to_all | solution.py:122
  171.5 6.2 %copy.37 = f32[64,8,16,128]{3,1,2,0:T(8,128)} copy(f32[64,8,16,128]{3,2,1,0:T(8,128)} %bitcast.42) | data formatting | bytes 8388608
  177.7 5.6 %copy.13 = f32[512,2048]{0,1:T(8,128)} copy(f32[512,2048]{1,0:T(8,128)} %bitcast.100) | data formatting | bytes 8388608 | tf_op jit(solution)/shard_map/reshape;reshape | solution.py:54
  183.2 13.2 %fusion.35 = f32[128,4,16,128]{3,0,2,1:T(8,128)S(1)} fusion(f32[16,128,512,1]{2,1,0,3:T(8,128)} %bitcast.99, s32[128,4]{0,1:T(4,128)S(1)} %multiply_add_fusion.1), kind=kOutput, calls=%fused_computation.69 | convolution fusion | flops 6446645248 | bytes 8390656 | tf_op jit(solution)/shard_map/dot_general | solution.py:55
  196.4 4.8 copy.14
  201.3 6.6 %all-to-all-start.1 = ((f32[128,4,16,128]{3,2,1,0:T(8,128)}), f32[128,4,16,128]{3,2,1,0:T(8,128)}, u32[]{:S(2)}, u32[]{:S(2)}) async-start(f32[128,4,16,128]{3,2,1,0:T(8,128)} %copy.14), calls=%async_computation.1 | async-start | bytes 8388608 | tf_op jit(solution)/shard_map/all_to_all | solution.py:127
  207.9 5.3 %slice_reduce_fusion = f32[]{:T(128)} fusion(f32[66,130,130]{2,1,0:T(8,128)} %copy-done), kind=kLoop, calls=%fused_computation.33 | loop fusion | flops 1048575 | bytes 4194308 | tf_op jit(solution)/shard_map/reduce_sum | solution.py:108
  213.2 43.7 %psum.35 = f32[]{:T(128)} all-reduce(f32[]{:T(128)} %slice_reduce_fusion), channel_id=1, replica_groups=mesh['gx'=4,'gy_0'=2,'gy_1'=2,'gz_0'=4,'gz_1'=2] {'gx'}, use_global_device_ids=true, to_apply=%region_1.2 | all-reduce | flops 1 | bytes 8 | tf_op jit(solution)/shard_map/psum | solution.py:36
  256.9 7.0 %psum.36 = f32[]{:T(128)} all-reduce(f32[]{:T(128)} %psum.35), channel_id=1, replica_groups=mesh['gx'=4,'gy_0'=2,'gy_1'=2,'gz_0'=4,'gz_1'=2] {'gy_0'}, use_global_device_ids=true, to_apply=%region_2.3 | all-reduce | flops 1 | bytes 8 | tf_op jit(solution)/shard_map/psum | solution.py:36
  264.0 3.1 psum.37
  267.2 12.4 %psum.38 = f32[]{:T(128)} all-reduce(f32[]{:T(128)} %psum.37), channel_id=1, replica_groups=mesh['gx'=4,'gy_0'=2,'gy_1'=2,'gz_0'=4,'gz_1'=2] {'gz_0'}, use_global_device_ids=true, to_apply=%region_4.5 | all-reduce | flops 1 | bytes 8 | tf_op jit(solution)/shard_map/psum | solution.py:36
  279.6 5.5 %psum.39 = f32[]{:T(128)} all-reduce(f32[]{:T(128)} %psum.38), channel_id=1, replica_groups=mesh['gx'=4,'gy_0'=2,'gy_1'=2,'gz_0'=4,'gz_1'=2] {'gz_1'}, use_global_device_ids=true, to_apply=%region_5.6 | all-reduce | flops 1 | bytes 8 | tf_op jit(solution)/shard_map/psum | solution.py:36
  285.7 6.9 %copy.38 = f32[4,4,8,4,16,128]{5,1,4,2,0,3:T(4,128)} copy(f32[4,4,8,4,16,128]{5,4,3,2,1,0:T(8,128)} %bitcast.15) | data formatting | bytes 8388608 | tf_op jit(solution)/shard_map/reshape | solution.py:128
  292.6 5.5 %reshape.227 = f32[4,512,512]{2,1,0:T(8,128)} reshape(f32[4,4,8,16,4,128]{5,4,3,2,1,0:T(4,128)} %bitcast.101) | data formatting | bytes 8388608 | tf_op jit(solution)/shard_map/reshape | solution.py:129
  298.1 20.0 %fusion.41 = f32[4,512,512]{2,1,0:T(8,128)S(1)} fusion(f32[4,512,512]{2,1,0:T(8,128)} %reshape.227), kind=kOutput, calls=%fused_computation.75 | convolution fusion | flops 6446645248 | bytes 8388608 | tf_op jit(solution)/shard_map/ij,rjy->riy/dot_general | solution.py:62
  318.1 20.1 %fusion.18 = f32[4,512,512]{2,1,0:T(8,128)S(1)} fusion(f32[4,512,512]{2,1,0:T(8,128)S(1)} %fusion.41), kind=kOutput, calls=%fused_computation.41 | convolution fusion | flops 6446645248 | bytes 8388608 | tf_op jit(solution)/shard_map/dot_general | solution.py:64
  338.3 13.2 %fusion.12 = f32[4,512,512]{1,2,0:T(8,128)S(1)} fusion(f32[4,512,512]{2,1,0:T(8,128)S(1)} %fusion.18, f32[512]{0:T(512)S(1)} %fusion.88, f32[4,512]{1,0:T(4,128)S(1)} %broadcast_add_fusion, f32[]{:T(128)S(6)} %mul_shard_map.3), kind=kOutput, calls=%fused_computation.30 | convolution fusion | flops 6451888128 | bytes 8398852 | tf_op jit(solution)/shard_map/ij,rjy->riy/dot_general | solution.py:62
  351.5 11.1 %convolution_bitcast_fusion = f32[4,4,8,4,16,128]{5,4,1,2,0,3:T(8,128)S(1)} fusion(f32[4,4,8,16,512,1]{4,3,5,2,1,0:T(8,128)S(1)} %bitcast.106, s32[4,128]{1,0:T(4,128)S(1)} %multiply_add_fusion), kind=kOutput, calls=%fused_computation.45 | convolution fusion | flops 6446645248 | bytes 8390656 | tf_op jit(solution)/shard_map/dot_general | solution.py:64
  363.2 59.6 %all_to_all.33 = f32[128,4,16,128]{3,2,1,0:T(8,128)S(1)} all-to-all(f32[128,4,16,128]{3,2,1,0:T(8,128)S(1)} %bitcast.102), channel_id=1, replica_groups=mesh['gx'=4,'gy_0'=2,'gy_1'=2,'gz_0'=4,'gz_1'=2] {'gx','gy_0','gy_1','gz..., dimensions={0} | all-to-all | bytes 8388608 | tf_op jit(solution)/shard_map/all_to_all | solution.py:134
  422.8 4.0 copy.36
  426.8 5.5 %copy.19 = f32[2048,512]{1,0:T(8,128)} copy(f32[2048,512]{0,1:T(8,128)} %bitcast.104) | data formatting | bytes 8388608 | tf_op jit(solution)/shard_map/dot_general | solution.py:55
  432.3 13.2 %fusion.37 = f32[512,16,128]{2,0,1:T(8,128)S(1)} fusion(f32[16,128,512]{2,1,0:T(8,128)} %bitcast.98), kind=kOutput, calls=%fused_computation.71 | convolution fusion | flops 6446645248 | bytes 8388608 | tf_op jit(solution)/shard_map/dot_general | solution.py:55
  445.5 2.4 copy.20
  447.9 51.2 %all_to_all.34 = f32[512,16,128]{2,1,0:T(8,128)S(1)} all-to-all(f32[512,16,128]{2,1,0:T(8,128)S(1)} %copy.20), channel_id=1, replica_groups=mesh['gx'=4,'gy_0'=2,'gy_1'=2,'gz_0'=4,'gz_1'=2] {'gz_0','gz_1'}, dimensions={0} | all-to-all | bytes 8388608 | tf_op jit(solution)/shard_map/all_to_all | solution.py:136
  499.1 2.6 copy.21
  (20 shorter events, 4.2 us)
Async XLA Ops:
  10.9 15.0 %collective-permute-start.1 = (f32[64,128,1]{1,0,2:T(8,128)S(1)}, f32[64,128,1]{1,0,2:T(8,128)S(1)}, u32[]{:S(2)}, u32[]{:S(2)}) collective-permute-start(f32[64,128,1]{1,0,2:T(8,128)S(1)} %copy.27), channel_id=1, source_target_pairs={{0,8},{8,16},{16,24},{24,0},{1,9},{9,17},{17,25},{25,1},{2,10},{10... | collective-permute-start | bytes 98312 | tf_op jit(solution)/shard_map/ppermute | solution.py:23
  13.8 16.7 %collective-permute-start.4 = (f32[64,128,1]{1,0,2:T(8,128)S(1)}, f32[64,128,1]{1,0,2:T(8,128)S(1)}, u32[]{:S(2)}, u32[]{:S(2)}) collective-permute-start(f32[64,128,1]{1,0,2:T(8,128)S(1)} %copy.28), channel_id=1, source_target_pairs={{8,0},{16,8},{24,16},{0,24},{9,1},{17,9},{25,17},{1,25},{10,2},{18... | collective-permute-start | bytes 98312 | tf_op jit(solution)/shard_map/ppermute | solution.py:24
  18.0 15.2 %collective-permute-start = (f32[1,128,128]{2,1,0:T(8,128)S(1)}, f32[1,128,128]{2,1,0:T(8,128)S(1)}, u32[]{:S(2)}, u32[]{:S(2)}) collective-permute-start(f32[1,128,128]{2,1,0:T(8,128)S(1)} %get-tuple-element.7), channel_id=1, source_target_pairs={{0,1},{1,2},{2,3},{3,4},{4,5},{5,6},{6,7},{7,0},{8,9},{9,10},{10,1... | collective-permute-start | bytes 196616 | tf_op jit(solution)/shard_map/ppermute | solution.py:23
  19.7 13.5 %collective-permute-start.5 = (f32[1,128,128]{2,1,0:T(8,128)S(1)}, f32[1,128,128]{2,1,0:T(8,128)S(1)}, u32[]{:S(2)}, u32[]{:S(2)}) collective-permute-start(f32[1,128,128]{2,1,0:T(8,128)S(1)} %get-tuple-element.8), channel_id=1, source_target_pairs={{1,0},{2,1},{3,2},{4,3},{5,4},{6,5},{7,6},{0,7},{9,8},{10,9},{11,1... | collective-permute-start | bytes 196616 | tf_op jit(solution)/shard_map/ppermute | solution.py:24
  24.3 8.8 %collective-permute-start.2 = (f32[64,1,128]{2,1,0:T(1,128)S(1)}, f32[64,1,128]{2,1,0:T(1,128)S(1)}, u32[]{:S(2)}, u32[]{:S(2)}) collective-permute-start(f32[64,1,128]{2,1,0:T(1,128)S(1)} %get-tuple-element.11), channel_id=1, source_target_pairs={{0,32},{32,64},{64,96},{96,0},{1,33},{33,65},{65,97},{97,1},{2,34}... | collective-permute-start | bytes 98312 | tf_op jit(solution)/shard_map/ppermute | solution.py:23
  25.9 7.2 %collective-permute-start.3 = (f32[64,1,128]{2,1,0:T(1,128)S(1)}, f32[64,1,128]{2,1,0:T(1,128)S(1)}, u32[]{:S(2)}, u32[]{:S(2)}) collective-permute-start(f32[64,1,128]{2,1,0:T(1,128)S(1)} %get-tuple-element.12), channel_id=1, source_target_pairs={{32,0},{64,32},{96,64},{0,96},{33,1},{65,33},{97,65},{1,97},{34,2}... | collective-permute-start | bytes 98312 | tf_op jit(solution)/shard_map/ppermute | solution.py:24
  48.9 34.8 %copy-start = (f32[66,130,130]{2,1,0:T(8,128)}, f32[66,130,130]{2,1,0:T(8,128)S(1)}, u32[]{:S(2)}) copy-start(f32[66,130,130]{2,1,0:T(8,128)S(1)} %get-tuple-element.5) | copy-start | bytes 13384804
  118.7 52.8 %all-to-all-start = ((f32[8,64,16,128]{3,2,1,0:T(8,128)}), f32[8,64,16,128]{3,2,1,0:T(8,128)}, u32[]{:S(2)}, u32[]{:S(2)}) async-start(f32[8,64,16,128]{3,2,1,0:T(8,128)} %fusion.66), calls=%async_computation | async-start | bytes 8388608 | tf_op jit(solution)/shard_map/all_to_all | solution.py:122
  201.3 84.4 %all-to-all-start.1 = ((f32[128,4,16,128]{3,2,1,0:T(8,128)}), f32[128,4,16,128]{3,2,1,0:T(8,128)}, u32[]{:S(2)}, u32[]{:S(2)}) async-start(f32[128,4,16,128]{3,2,1,0:T(8,128)} %copy.14), calls=%async_computation.1 | async-start | bytes 8388608 | tf_op jit(solution)/shard_map/all_to_all | solution.py:127
